TPU v7x, 256 devices: a whole 4x4x8 slice. The times are simulated.
256 devices in a mesh: tok: 8 (over z_hi, x), head: 32 (over y, z_lo, core).
Axes of the slice: x: 4, y: 4, z: 8 (z_hi: 2, z_lo: 4; z = z_hi * 4 + z_lo), core: 2. Of those that a mesh axis runs over, the one named last changes fastest.
Arguments:
- query_states: bfloat16 [16384, 8192], P(('tok', 'head')), may hold values from -7.5 to 7.5
- key_states: bfloat16 [16384, 8192], P(('tok', 'head')), may hold values from -7.5 to 7.5
- value_states: bfloat16 [16384, 8192], P(('tok', 'head')), may hold values from -6 to 6
- token_rates: float32 [32, 16384], P('head', 'tok'), may hold values from 0.05 to 1
- fast_weights: bfloat16 [32, 512, 768], P('head'), may hold values from -0.375 to 0.375
Outputs:
- combined: bfloat16 [16384, 8192], P(('tok', 'head'))
- new_weights: bfloat16 [32, 512, 768], P('head', 'tok')
All inputs are finite; a program needn't handle non-finite values.
Results may differ from a plain program's by a relative error of at most 0.039.
Values may be sent and summed in bfloat16 or wider, within the bound.
No kernel may reach another device: no remote copies, remote signals or barrier semaphores. Data moves between devices by JAX's collectives and lax.ppermute only.
A program may use at most 64 MiB of HBM per device.

v0:
```python
import jax
import jax.numpy as jnp
from jax import lax
from jax.sharding import Mesh
from jax.sharding import PartitionSpec as P

DH = 256
FH = 512
WINDOW = 1024
NS_STEPS = 5
TOK = ("tok_0", "tok_1")
TOK_HEAD = ("tok_0", "tok_1", "head")


coef_linear = 3.4445
coef_cubic = -4.775
coef_quintic = 2.0315
epsilon = 1e-06


def shifted(value, axis, steps):
    count = lax.axis_size(axis)
    first, last = (max(0, -steps), min(count, count - steps))
    return lax.ppermute(value, axis, [(source, source + steps) for source in range(first, last)])


def padded_to(lines, devices):
    spare = -lines.shape[0] % devices
    if not spare:
        return lines
    return jnp.concatenate([lines, jnp.zeros((spare, *lines.shape[1:]), lines.dtype)])


def own_block(pieces, axes, sequence):
    shape = [lax.axis_size(a) for a in axes]
    pieces = pieces.reshape(*shape, *pieces.shape[1:])
    pieces = pieces.transpose(*sequence, *range(len(axes), pieces.ndim))
    pieces = pieces.reshape(-1, *pieces.shape[len(axes) :])
    for k in sequence:
        pieces = lax.psum_scatter(pieces, axes[k], scatter_dimension=0, tiled=True)
    return pieces[0]


def all_blocks(shard, axes, sequence):
    pieces = shard[None]
    for k in sequence:
        pieces = lax.all_gather(pieces, axes[k], axis=0, tiled=True)
    current = [lax.axis_size(axes[k]) for k in reversed(sequence)]
    pieces = pieces.reshape(*current, *shard.shape)
    turned = sorted(range(len(sequence)), key=lambda place: sequence[len(sequence) - 1 - place])
    return pieces.transpose(*turned, *range(len(sequence), pieces.ndim)).reshape(-1, *shard.shape)


def sum_in_two_steps(shard, axes, sequence):
    devices, lines = (lax.axis_size(axes), shard.reshape(-1, *shard.shape[1:][-1:]))
    pieces = padded_to(lines, devices).reshape(devices, -1, *lines.shape[1:])
    own = own_block(pieces, axes, sequence)
    whole = all_blocks(own, axes, sequence[::-1]).reshape(-1, *lines.shape[1:])
    return whole[: len(lines)].reshape(shard.shape)


def block_size():
    return 512


def rms_norm(values):
    return values * lax.rsqrt(jnp.mean(values * values, axis=-1, keepdims=True) + epsilon)


def silu_parts(gate_value):
    sigmoid = jax.nn.sigmoid(gate_value)
    return (gate_value * sigmoid, sigmoid * (1.0 + gate_value * (1.0 - sigmoid)))


def across(inputs, weight_rows):
    return lax.dot_general(
        inputs, weight_rows, (((1,), (1,)), ((), ())), preferred_element_type=jnp.float32
    )


def apply_rows(query_rows, weight_rows):
    query_gate = across(query_rows, weight_rows[:, :DH])
    query_up = across(query_rows, weight_rows[:, DH : 2 * DH])
    query_hidden = (jax.nn.silu(query_gate) * query_up).astype(jnp.bfloat16)
    return jnp.dot(query_hidden, weight_rows[:, 2 * DH :], preferred_element_type=jnp.float32)


def attend(query_rows, key_rows, value_rows, positions, key_positions):
    scores = jnp.dot(query_rows, key_rows.T, preferred_element_type=jnp.float32) * DH ** (-0.5)
    offset = positions[:, None] - key_positions[None, :]
    allowed = (offset >= 0) & (offset < WINDOW) & (key_positions[None, :] >= 0)
    scores = jnp.where(allowed, scores, -1e30)
    highest = jnp.max(scores, axis=1, keepdims=True)
    expo = jnp.exp(scores - highest)
    probs = (expo / jnp.sum(expo, axis=1, keepdims=True)).astype(jnp.bfloat16)
    return jnp.dot(probs, value_rows, preferred_element_type=jnp.float32)


def polish(iterate, gram_matrix):
    square_gram = jnp.einsum(
        "jde,jef->jdf", gram_matrix, gram_matrix, preferred_element_type=jnp.float32
    )
    polynomial = (coef_cubic * gram_matrix.astype(jnp.float32) + coef_quintic * square_gram).astype(
        jnp.bfloat16
    )
    product = jnp.einsum("fjd,jde->fje", iterate, polynomial, preferred_element_type=jnp.float32)
    return (coef_linear * iterate.astype(jnp.float32) + product).astype(jnp.bfloat16)


def per_device(query_states, key_states, value_states, token_rates, fast_weights):
    query_rows, key_rows, value_rows = (
        lax.all_to_all(query_states, "head", split_axis=1, concat_axis=0, tiled=True),
        lax.all_to_all(key_states, "head", split_axis=1, concat_axis=0, tiled=True),
        lax.all_to_all(value_states, "head", split_axis=1, concat_axis=0, tiled=True),
    )
    local_rows = query_rows.shape[0]
    tok_index = lax.axis_index(TOK)
    tok_count = lax.axis_size(TOK)
    previous = shifted((key_rows[local_rows - WINDOW :], value_rows[local_rows - WINDOW :]), TOK, 1)
    window_key_rows = jnp.concatenate([previous[0], key_rows])
    window_value_rows = jnp.concatenate([previous[1], value_rows])
    block_rows = block_size()
    first_position = tok_index * local_rows

    def attend_block(block_index):
        offset = block_index * block_rows
        queries_here = lax.dynamic_slice_in_dim(query_rows, offset, block_rows, 0)
        keys_here = lax.dynamic_slice_in_dim(window_key_rows, offset, block_rows + WINDOW, 0)
        values_here = lax.dynamic_slice_in_dim(window_value_rows, offset, block_rows + WINDOW, 0)
        positions = first_position + offset + jnp.arange(block_rows, dtype=jnp.int32)
        key_positions = (
            first_position + offset - WINDOW + jnp.arange(block_rows + WINDOW, dtype=jnp.int32)
        )
        return attend(queries_here, keys_here, values_here, positions, key_positions)

    attended = lax.map(attend_block, jnp.arange(local_rows // block_rows, dtype=jnp.int32)).reshape(
        local_rows, DH
    )
    attended = rms_norm(attended)
    weights = fast_weights[0]
    rate_rows = token_rates[0]
    gate_value = across(key_rows, weights[:, :DH])
    up_value = across(key_rows, weights[:, DH : 2 * DH])
    gate_silu, gate_slope = silu_parts(gate_value)
    hidden = (gate_silu * up_value).astype(jnp.bfloat16)
    target = (-rate_rows[:, None] * value_rows.astype(jnp.float32)).astype(jnp.bfloat16)
    back_grad = across(target, weights[:, 2 * DH :])
    gate_grad = (back_grad * up_value * gate_slope).astype(jnp.bfloat16)
    up_grad = (back_grad * gate_silu).astype(jnp.bfloat16)
    owned_rows = FH // tok_count

    def outer(left):
        return lax.dot_general(
            left,
            key_rows if left is not hidden else target,
            (((0,), (0,)), ((), ())),
            preferred_element_type=jnp.float32,
        )

    gradient = (
        sum_in_two_steps(
            jnp.concatenate([outer(gate_grad), outer(up_grad), outer(hidden)], axis=1).astype(
                jnp.bfloat16
            ),
            TOK,
            (1, 0),
        )
        .astype(jnp.float32)
        .reshape(FH, 3, DH)
    )
    squares = jnp.sum(gradient * gradient, axis=(0, 2))
    iterate = (gradient * lax.rsqrt(squares + epsilon)[None, :, None]).astype(jnp.bfloat16)
    for repeat_index in range(NS_STEPS):
        gram_matrix = jnp.einsum(
            "fjd,fje->jde", iterate, iterate, preferred_element_type=jnp.float32
        ).astype(jnp.bfloat16)
        iterate = polish(iterate, gram_matrix)
    updated = (
        (weights.reshape(FH, 3, DH).astype(jnp.float32) - iterate.astype(jnp.float32))
        .astype(jnp.bfloat16)
        .reshape(FH, 3 * DH)
    )
    owned_weights = lax.dynamic_slice_in_dim(updated, tok_index * owned_rows, owned_rows, 0)
    applied = apply_rows(query_rows, updated)
    combined = (attended + rms_norm(applied)).astype(jnp.bfloat16)
    combined = lax.all_to_all(combined, "head", split_axis=0, concat_axis=1, tiled=True)
    return (combined, owned_weights[None])


def solution(mesh):
    finer = Mesh(mesh.devices.reshape(2, 4, mesh.shape["head"]), ("tok_0", "tok_1", "head"))
    return jax.shard_map(
        per_device,
        mesh=finer,
        in_specs=(
            P(TOK_HEAD, None),
            P(TOK_HEAD, None),
            P(TOK_HEAD, None),
            P("head", TOK),
            P("head", None, None),
        ),
        out_specs=(P(TOK_HEAD, None), P("head", TOK, None)),
        check_vma=False,
    )
```

profile of v0, /device:TPU:1, one launch (start us, length us, event | category | flops | bytes accessed | tf_op | source)
XLA Modules:
  0.0 281.4 jit_solution(13374684359710127897)
XLA Ops:
  7.2 2.4 copy.128
  9.6 10.2 %all-to-all-start.1 = ((bf16[64,32,256]{2,0,1:T(8,128)(2,1)}), bf16[64,32,256]{2,0,1:T(8,128)(2,1)S(1)}, u32[]{:S(2)}, u32[]{:S(2)}) async-start(bf16[64,32,256]{2,0,1:T(8,128)(2,1)} %bitcast.153), calls=%async_computation.1 | async-start | bytes 2097152 | tf_op jit(solution)/shard_map/all_to_all | solution.py:113
  19.8 1.1 copy.127
  20.9 26.7 %all-to-all-done.1 = bf16[64,32,256]{2,0,1:T(8,128)(2,1)S(1)} async-done(((bf16[64,32,256]{2,0,1:T(8,128)(2,1)}), bf16[64,32,256]{2,0,1:T(8,128)(2,1)S(1)}, u32[]{:S(2)}, u32[]{:S(2)}) %all-to-all-start.1) | async-done | bytes 1048608 | tf_op jit(solution)/shard_map/all_to_all | solution.py:113
  47.6 3.9 %all-to-all-start.2 = ((bf16[64,32,256]{2,0,1:T(8,128)(2,1)}), bf16[64,32,256]{2,0,1:T(8,128)(2,1)S(1)}, u32[]{:S(2)}, u32[]{:S(2)}) async-start(bf16[64,32,256]{2,0,1:T(8,128)(2,1)} %bitcast.152), calls=%async_computation.2 | async-start | bytes 2097152 | tf_op jit(solution)/shard_map/all_to_all | solution.py:114
  51.6 1.4 copy.79
  53.1 2.3 copy.129
  55.4 3.9 %collective-permute-start = (bf16[1024,256]{1,0:T(8,128)(2,1)S(1)}, bf16[1024,256]{1,0:T(8,128)(2,1)}, u32[]{:S(2)}, u32[]{:S(2)}) collective-permute-start(bf16[1024,256]{1,0:T(8,128)(2,1)S(1)} %bitcast.183), channel_id=1, source_target_pairs={{0,32},{32,64},{64,96},{96,128},{128,160},{160,192},{192,224},{1,3... | collective-permute-start | bytes 1572872 | tf_op jit(solution)/shard_map/ppermute | solution.py:24
  59.4 20.0 %all-to-all-done.2 = bf16[64,32,256]{2,0,1:T(8,128)(2,1)S(1)} async-done(((bf16[64,32,256]{2,0,1:T(8,128)(2,1)}), bf16[64,32,256]{2,0,1:T(8,128)(2,1)S(1)}, u32[]{:S(2)}, u32[]{:S(2)}) %all-to-all-start.2) | async-done | bytes 1048608 | tf_op jit(solution)/shard_map/all_to_all | solution.py:114
  79.4 4.5 %all-to-all-start = ((bf16[64,32,256]{2,0,1:T(8,128)(2,1)}), bf16[64,32,256]{2,0,1:T(8,128)(2,1)}, u32[]{:S(2)}, u32[]{:S(2)}) async-start(bf16[64,32,256]{2,0,1:T(8,128)(2,1)} %bitcast.154), calls=%async_computation | async-start | bytes 2097152 | tf_op jit(solution)/shard_map/all_to_all | solution.py:112
  83.9 0.9 slice.41
  84.8 3.9 %collective-permute-start.1 = (bf16[1024,256]{1,0:T(8,128)(2,1)}, bf16[1024,256]{1,0:T(8,128)(2,1)}, u32[]{:S(2)}, u32[]{:S(2)}) collective-permute-start(bf16[1024,256]{1,0:T(8,128)(2,1)} %bitcast.8), channel_id=1, source_target_pairs={{0,32},{32,64},{64,96},{96,128},{128,160},{160,192},{192,224},{1,3... | collective-permute-start | bytes 1572872 | tf_op jit(solution)/shard_map/ppermute | solution.py:24
  88.7 0.7 fusion.65
  89.5 0.8 fusion.38
  90.3 2.7 fusion.17
  93.0 0.7 convolution_convert_fusion.6
  93.8 0.7 convolution_convert_fusion.7
  94.8 0.7 convolution_convert_fusion.5
  95.6 0.9 copy.80
  96.6 2.3 pad_maximum_fusion
  99.1 2.5 pad_maximum_fusion.1
  101.5 10.3 %all-to-all-done = bf16[64,32,256]{2,0,1:T(8,128)(2,1)} async-done(((bf16[64,32,256]{2,0,1:T(8,128)(2,1)}), bf16[64,32,256]{2,0,1:T(8,128)(2,1)}, u32[]{:S(2)}, u32[]{:S(2)}) %all-to-all-start) | async-done | bytes 1048608 | tf_op jit(solution)/shard_map/all_to_all | solution.py:112
  111.9 23.9 %while.12 = (s32[]{:T(128)}, f32[4,512,256]{2,1,0:T(8,128)S(1)}, s32[4]{0:T(128)S(1)}, s32[]{:T(128)}, bf16[2048,256]{1,0:T(8,128)(2,1)}, /*index=5*/bf16[3072,2...) while((s32[]{:T(128)}, f32[4,512,256]{2,1,0:T(8,128)S(1)}, ...), condition=%wide.region_3.4_spmd, body=%wide.region_0.3_spmd.sunk | while | flops 815534080 | bytes 18117920 | solution.py:136
  113.2 2.5 fusion.122
  116.3 0.8 copy-done.5
  117.1 0.7 fusion.124
  119.2 2.5 fusion.122
  122.3 0.9 copy-done.5
  123.1 0.7 fusion.124
  125.1 2.5 fusion.122
  128.2 0.9 copy-done.5
  131.1 2.5 fusion.122
  134.2 0.8 copy-done.5
  136.2 49.4 %reduce-scatter.5.cloned.1.call-done = bf16[1,64,768]{2,1,0:T(8,128)(2,1)} async-done(((bf16[2,64,768]{2,1,0:T(8,128)(2,1)}), bf16[1,64,768]{2,1,0:T(8,128)(2,1)}) %reduce-scatter.5.cloned.1.call-update) | async-done | bytes 98320 | tf_op jit(solution)/shard_map/reduce_scatter | solution.py:40
  185.7 8.3 %all_gather.6 = bf16[2,64,768]{2,1,0:T(8,128)(2,1)S(1)} all-gather(bf16[1,64,768]{2,1,0:T(8,128)(2,1)} %reduce-scatter.5.cloned.1.call-done), channel_id=1, replica_groups=mesh['tok_0'=2,'tok_1'=4,'head'=32] {'tok_0'}, dimensions={0}, use_global_device_ids=true | all-gather | bytes 294912 | tf_op jit(solution)/shard_map/all_gather | solution.py:47
  194.0 10.8 %all_gather.7 = bf16[8,64,768]{2,1,0:T(8,128)(2,1)S(1)} all-gather(bf16[2,64,768]{2,1,0:T(8,128)(2,1)S(1)} %all_gather.6), channel_id=1, replica_groups=mesh['tok_0'=2,'tok_1'=4,'head'=32] {'tok_1'}, dimensions={0}, use_global_device_ids=true | all-gather | bytes 983040 | tf_op jit(solution)/shard_map/all_gather | solution.py:47
  204.8 1.3 convert_element_type.196
  206.3 3.1 %copy.117 = f32[2,4,64,768]{2,1,0,3:T(4,128)S(1)} copy(f32[2,4,64,768]{3,2,0,1:T(8,128)} %bitcast.169) | data formatting | bytes 3145728 | tf_op jit(solution)/shard_map/convert_element_type | solution.py:168
  209.5 2.9 %reshape.113 = f32[512,3,256]{0,2,1:T(8,128)} reshape(f32[2,4,64,768]{2,1,0,3:T(4,128)S(1)} %copy.117) | data formatting | bytes 3145728 | tf_op jit(solution)/shard_map/convert_element_type | solution.py:168
  212.5 2.4 convolution_convert_fusion.4
  214.9 2.5 fusion.26
  221.8 3.9 %fusion.63 = f32[512,2048]{1,0:T(8,128)} fusion(bf16[2048,256]{1,0:T(8,128)(2,1)} %bitcast.3, bf16[512,768]{0,1:T(8,128)(2,1)S(1)} %bitcast.172), kind=kOutput, calls=%fused_computation.109 | convolution fusion | flops 536870912 | bytes 5505024 | tf_op jit(solution)/shard_map/dot_general | solution.py:76
  225.8 6.0 %multiply_reduce_fusion = (f32[2048]{0:T(1024)S(1)}, f32[2048,256]{1,0:T(8,128)}) fusion(bf16[512,768]{0,1:T(8,128)(2,1)S(1)} %bitcast.173, f32[512,2048]{1,0:T(8,128)} %fusion.63, bf16[2048,256]{1,0:T(8,128)(2,1)} %bitcast.3), kind=kOutput, calls=%fused_computation.38 | convolution fusion | flops 1081079808 | bytes 7872512 | tf_op jit(solution)/shard_map/dot_general | solution.py:85
  231.8 2.8 fusion.21
  234.6 11.1 %all-to-all-start.3 = ((bf16[32,64,256]{2,1,0:T(8,128)(2,1)}), bf16[32,64,256]{2,1,0:T(8,128)(2,1)S(1)}, u32[]{:S(2)}, u32[]{:S(2)}) async-start(bf16[32,64,256]{2,1,0:T(8,128)(2,1)} %bitcast.40), calls=%async_computation.5 | async-start | bytes 2097152 | tf_op jit(solution)/shard_map/all_to_all | solution.py:186
  245.8 0.8 copy.99
  246.6 26.9 %all-to-all-done.3 = bf16[32,64,256]{2,1,0:T(8,128)(2,1)S(1)} async-done(((bf16[32,64,256]{2,1,0:T(8,128)(2,1)}), bf16[32,64,256]{2,1,0:T(8,128)(2,1)S(1)}, u32[]{:S(2)}, u32[]{:S(2)}) %all-to-all-start.3) | async-done | bytes 1048608 | tf_op jit(solution)/shard_map/all_to_all | solution.py:186
  273.5 1.0 copy.122
  (71 shorter events, 12.1 us)
Async XLA Ops:
  7.2 12.6 %copy-start.6 = (bf16[64,8192]{1,0:T(8,128)(2,1)S(1)}, bf16[64,8192]{1,0:T(8,128)(2,1)}, u32[]{:S(2)}) copy-start(bf16[64,8192]{1,0:T(8,128)(2,1)} %param.9) | copy-start | bytes 3145732
  9.6 38.0 %all-to-all-start.1 = ((bf16[64,32,256]{2,0,1:T(8,128)(2,1)}), bf16[64,32,256]{2,0,1:T(8,128)(2,1)S(1)}, u32[]{:S(2)}, u32[]{:S(2)}) async-start(bf16[64,32,256]{2,0,1:T(8,128)(2,1)} %bitcast.153), calls=%async_computation.1 | async-start | bytes 2097152 | tf_op jit(solution)/shard_map/all_to_all | solution.py:113
  19.8 31.7 %copy-start.7 = (f32[1,2048]{1,0:T(1,128)S(1)}, f32[1,2048]{1,0:T(1,128)}, u32[]{:S(2)}) copy-start(f32[1,2048]{1,0:T(1,128)} %param.10) | copy-start | bytes 24580
  19.8 31.8 %copy-start.4 = (bf16[1,512,768]{2,1,0:T(8,128)(2,1)S(1)}, bf16[1,512,768]{2,1,0:T(8,128)(2,1)}, u32[]{:S(2)}) copy-start(bf16[1,512,768]{2,1,0:T(8,128)(2,1)} %param.11) | copy-start | bytes 2359300
  47.6 31.8 %all-to-all-start.2 = ((bf16[64,32,256]{2,0,1:T(8,128)(2,1)}), bf16[64,32,256]{2,0,1:T(8,128)(2,1)S(1)}, u32[]{:S(2)}, u32[]{:S(2)}) async-start(bf16[64,32,256]{2,0,1:T(8,128)(2,1)} %bitcast.152), calls=%async_computation.2 | async-start | bytes 2097152 | tf_op jit(solution)/shard_map/all_to_all | solution.py:114
  55.4 41.2 %collective-permute-start = (bf16[1024,256]{1,0:T(8,128)(2,1)S(1)}, bf16[1024,256]{1,0:T(8,128)(2,1)}, u32[]{:S(2)}, u32[]{:S(2)}) collective-permute-start(bf16[1024,256]{1,0:T(8,128)(2,1)S(1)} %bitcast.183), channel_id=1, source_target_pairs={{0,32},{32,64},{64,96},{96,128},{128,160},{160,192},{192,224},{1,3... | collective-permute-start | bytes 1572872 | tf_op jit(solution)/shard_map/ppermute | solution.py:24
  79.4 32.5 %all-to-all-start = ((bf16[64,32,256]{2,0,1:T(8,128)(2,1)}), bf16[64,32,256]{2,0,1:T(8,128)(2,1)}, u32[]{:S(2)}, u32[]{:S(2)}) async-start(bf16[64,32,256]{2,0,1:T(8,128)(2,1)} %bitcast.154), calls=%async_computation | async-start | bytes 2097152 | tf_op jit(solution)/shard_map/all_to_all | solution.py:112
  83.9 51.9 %reduce-scatter.3.cloned.1.call-start = ((), (), s32[]{:S(2)}) async-start(), calls=%async_computation.6 | async-start | bytes 983040 | tf_op jit(solution)/shard_map/reduce_scatter | solution.py:40
  84.8 14.3 %collective-permute-start.1 = (bf16[1024,256]{1,0:T(8,128)(2,1)}, bf16[1024,256]{1,0:T(8,128)(2,1)}, u32[]{:S(2)}, u32[]{:S(2)}) collective-permute-start(bf16[1024,256]{1,0:T(8,128)(2,1)} %bitcast.8), channel_id=1, source_target_pairs={{0,32},{32,64},{64,96},{96,128},{128,160},{160,192},{192,224},{1,3... | collective-permute-start | bytes 1572872 | tf_op jit(solution)/shard_map/ppermute | solution.py:24
  96.6 89.1 %reduce-scatter.5.cloned.1.call-start = ((), (), s32[]{:S(2)}) async-start(), calls=%async_computation.7 | async-start | bytes 294912 | tf_op jit(solution)/shard_map/reduce_scatter | solution.py:40
  98.9 13.0 %copy-start = (f32[4,512,256]{2,1,0:T(8,128)S(1)}, f32[4,512,256]{2,1,0:T(8,128)}, u32[]{:S(2)}) copy-start(f32[4,512,256]{2,1,0:T(8,128)} %custom-call) | copy-start | bytes 6291460
  115.7 1.4 copy-start.5
  121.7 1.4 copy-start.5
  127.7 1.4 copy-start.5
  133.7 1.4 copy-start.5
  135.8 70.3 %copy-start.1 = (f32[4,512,256]{2,1,0:T(8,128)}, f32[4,512,256]{2,1,0:T(8,128)S(1)}, u32[]{:S(2)}) copy-start(f32[4,512,256]{2,1,0:T(8,128)S(1)} %get-tuple-element.91) | copy-start | bytes 6291460
  219.8 1.4 copy-start.3
  225.8 6.0 %copy-start.2 = (f32[4,512,256]{2,1,0:T(8,128)S(1)}, f32[4,512,256]{2,1,0:T(8,128)}, u32[]{:S(2)}) copy-start(f32[4,512,256]{2,1,0:T(8,128)} %copy-done.1) | copy-start | bytes 6291460
  234.6 38.9 %all-to-all-start.3 = ((bf16[32,64,256]{2,1,0:T(8,128)(2,1)}), bf16[32,64,256]{2,1,0:T(8,128)(2,1)S(1)}, u32[]{:S(2)}, u32[]{:S(2)}) async-start(bf16[32,64,256]{2,1,0:T(8,128)(2,1)} %bitcast.40), calls=%async_computation.5 | async-start | bytes 2097152 | tf_op jit(solution)/shard_map/all_to_all | solution.py:186
Sparse Core Ops, SparseCore 0:
  96.7 32.4 reduce-scatter.2
  136.0 49.6 reduce-scatter.4
where the time goes:
time: 283 us; the launch traced here: 281 us
  waiting for transfers between devices  134 us (47%)
  matrix products  38.2 us (13%)
  starting transfers between devices  37.5 us (13%)
  local copies, waits for them, and re-layouts  23.3 us (8%)
  blocking collectives  19.2 us (7%)
  between operations  14.4 us (5%)
  other arithmetic  12.3 us (4%)
  loops' own time  2.85 us (1%)
    reduce_scatter x2, waiting for transfers between devices, own_block(): pieces = lax.psum_scatter(pieces, axes[k], scatter_dimension=0, tiled=True)  49.5 us
    all_to_all x1, waiting for transfers between devices, per_device(): lax.all_to_all(combined, 'head', split_axis=0, concat_axis=1, tiled=True)  26.9 us
    all_to_all x1, waiting for transfers between devices, per_device(): lax.all_to_all(key_states, 'head', split_axis=1, concat_axis=0, tiled=True)  26.7 us
    all_to_all x1, waiting for transfers between devices, per_device(): lax.all_to_all(value_states, 'head', split_axis=1, concat_axis=0, tiled=T...  20 us
    all_gather x2, blocking collectives, all_blocks(): pieces = lax.all_gather(pieces, axes[k], axis=0, tiled=True)  19.2 us
    all_to_all x1, starting transfers between devices, per_device(): lax.all_to_all(combined, 'head', split_axis=0, concat_axis=1, tiled=True)  11.1 us
    all_to_all x1, waiting for transfers between devices, per_device(): lax.all_to_all(query_states, 'head', split_axis=1, concat_axis=0, tiled=T...  10.3 us
    all_to_all x1, starting transfers between devices, per_device(): lax.all_to_all(key_states, 'head', split_axis=1, concat_axis=0, tiled=True)  10.2 us
  transfers between devices with their start and end apart: 8, of which 6 were waited for; matrix products, arithmetic and copies ran while one was open for 13% of the time, Pallas kernels for 0%

commit v1 on v0

v1 whole, which is shorter than its diff:
```python
import functools

import jax
import jax.numpy as jnp
from jax import lax
from jax.experimental import pallas as pl
from jax.experimental.pallas import tpu as pltpu
from jax.sharding import Mesh
from jax.sharding import PartitionSpec as P

DH = 256
FH = 512
WINDOW = 1024
NS_STEPS = 5
TOK = ("tok_0", "tok_1")
TOK_HEAD = ("tok_0", "tok_1", "head")
RING = 4
PIECE = 3 * DH // RING

coef_linear = 3.4445
coef_cubic = -4.775
coef_quintic = 2.0315
epsilon = 1e-06

F32 = jnp.float32
BF16 = jnp.bfloat16
LOG2E = 1.4426950408889634
SCALE2 = DH ** (-0.5) * LOG2E


def mm_nt(a, b):
    return lax.dot_general(a, b, (((1,), (1,)), ((), ())), preferred_element_type=F32)


def mm_tn(a, b):
    return lax.dot_general(a, b, (((0,), (0,)), ((), ())), preferred_element_type=F32)


def mm(a, b):
    return jnp.dot(a, b, preferred_element_type=F32)


def sigmoid(x):
    return 0.5 * jnp.tanh(0.5 * x) + 0.5


def rms_norm(values):
    return values * lax.rsqrt(jnp.mean(values * values, axis=-1, keepdims=True) + epsilon)


def gradient_kernel(index_ref, kv_ref, w_ref, r_ref, own_ref, s1_ref, s2_ref, s3_ref, acc_ref):
    rates = r_ref[...].T
    chunk = 8
    rows = chunk * 64
    for c in range(32 // chunk):
        keys = kv_ref[c * chunk : (c + 1) * chunk, 0:64, :].reshape(rows, DH)
        values = kv_ref[c * chunk : (c + 1) * chunk, 64:128, :].reshape(rows, DH).astype(F32)
        groups = rows // 128
        target = jnp.concatenate(
            [
                (-rates[:, groups * c + j : groups * c + j + 1] * values[j * 128 : (j + 1) * 128])
                for j in range(groups)
            ],
            axis=0,
        ).astype(BF16)
        gate = mm_nt(keys, w_ref[:, 0:DH])
        up = mm_nt(keys, w_ref[:, DH : 2 * DH])
        back = mm_nt(target, w_ref[:, 2 * DH : 3 * DH])
        s = sigmoid(gate)
        silu = gate * s
        hidden = (silu * up).astype(BF16)
        gate_grad = (back * up * (s * (1.0 + gate * (1.0 - s)))).astype(BF16)
        up_grad = (back * silu).astype(BF16)
        parts = (mm_tn(keys, gate_grad), mm_tn(keys, up_grad), mm_tn(target, hidden))
        for b in range(3):
            if c == 0:
                acc_ref[b * DH : (b + 1) * DH, :] = parts[b]
            else:
                acc_ref[b * DH : (b + 1) * DH, :] += parts[b]
    x = index_ref[1]
    for d, ref in enumerate((own_ref, s1_ref, s2_ref, s3_ref)):
        start = pl.multiple_of(((x + d) & (RING - 1)) * PIECE, PIECE)
        ref[...] = acc_ref[pl.ds(start, PIECE), :].astype(ref.dtype)


def gradient_pieces(index, kv, weights, rates):
    vmem = pl.BlockSpec(memory_space=pltpu.VMEM)
    piece = jax.ShapeDtypeStruct((PIECE, FH), BF16)
    return pl.pallas_call(
        gradient_kernel,
        in_specs=[pl.BlockSpec(memory_space=pltpu.SMEM), vmem, vmem, vmem],
        out_specs=[vmem] * 4,
        out_shape=[jax.ShapeDtypeStruct((PIECE, FH), F32), piece, piece, piece],
        scratch_shapes=[pltpu.VMEM((3 * DH, FH), F32)],
        compiler_params=pltpu.CompilerParams(vmem_limit_bytes=40 * 2**20),
        cost_estimate=pl.CostEstimate(flops=6 * 2 * 2048 * DH * FH, bytes_accessed=4 * 2**20, transcendentals=2**20),
        name="gradient",
    )(index, kv, weights, rates)


def attention_kernel(index_ref, q_ref, prev_ref, own_ref, out_ref, *, check):
    row = lax.broadcasted_iota(jnp.int32, (DH, DH), 0)
    col = lax.broadcasted_iota(jnp.int32, (DH, DH), 1)
    bias = jnp.where(index_ref[0] > 0, 0.0, -1e30).astype(F32)

    def piece(j, lo):
        ref, at = (prev_ref, 4 * j) if j < 4 else (own_ref, 4 * (j - 4))
        return ref[at : at + 4, lo : lo + 64, :].reshape(256, DH)

    for b in range(4):
        queries = q_ref[4 * b : 4 * b + 4].reshape(256, DH)
        scores = []
        for j in range(5):
            s = mm_nt(queries, piece(b + j, 0))
            if check and b + j < 4:
                s = s + bias
            if j == 0:
                s = jnp.where(col > row, s, -1e30)
            if j == 4:
                s = jnp.where(col <= row, s, -1e30)
            scores.append(s)
        top = functools.reduce(jnp.maximum, scores)
        highest = jnp.max(top, axis=1, keepdims=True)
        expo = [jnp.exp2((s - highest) * SCALE2) for s in scores]
        total = jnp.sum(functools.reduce(jnp.add, expo), axis=1, keepdims=True)
        probs = jnp.concatenate([e.astype(BF16) for e in expo], axis=1)
        values = jnp.concatenate([piece(b + j, 64) for j in range(5)], axis=0)
        out_ref[b * 256 : (b + 1) * 256, :] = rms_norm(mm(probs, values) / total)


def attention(index, query_rows, half, prev, prev_block, own, own_block, check):
    def whole(block):
        return lambda step: (block, 0, 0)

    return pl.pallas_call(
        functools.partial(attention_kernel, check=check),
        grid=(1,),
        in_specs=[
            pl.BlockSpec(memory_space=pltpu.SMEM),
            pl.BlockSpec((16, 64, DH), whole(half)),
            pl.BlockSpec((16, 128, DH), whole(prev_block)),
            pl.BlockSpec((16, 128, DH), whole(own_block)),
        ],
        out_specs=pl.BlockSpec((1024, DH), lambda step: (0, 0)),
        out_shape=jax.ShapeDtypeStruct((1024, DH), F32),
        compiler_params=pltpu.CompilerParams(vmem_limit_bytes=40 * 2**20),
        cost_estimate=pl.CostEstimate(flops=4 * 1024 * 1280 * DH, bytes_accessed=4 * 2**20, transcendentals=1024 * 1280),
        name="attention",
    )(index, query_rows, prev, own)


def update_kernel(index_ref, p0_ref, p1_ref, p2_ref, p3_ref, w_ref, q_ref, first_ref, second_ref, out_ref, nw_ref, y_ref, w2_ref):
    x = index_ref[1]
    for d, ref in enumerate((p0_ref, p1_ref, p2_ref, p3_ref)):
        start = pl.multiple_of(((x + RING - d) & (RING - 1)) * PIECE, PIECE)
        y_ref[pl.ds(start, PIECE), :] = ref[...]
    iterates = []
    for b in range(3):
        g = y_ref[b * DH : (b + 1) * DH, :].astype(F32)
        iterates.append((g * lax.rsqrt(jnp.sum(g * g, keepdims=True) + epsilon)).astype(BF16))
    for step in range(NS_STEPS):
        grams = [mm_nt(y, y).astype(BF16) for y in iterates]
        squares = [mm(a, a) for a in grams]
        polys = [(coef_cubic * a.astype(F32) + coef_quintic * s).astype(BF16) for a, s in zip(grams, squares)]
        iterates = [(coef_linear * y.astype(F32) + mm(p, y)).astype(BF16) for p, y in zip(polys, iterates)]
    for b in range(3):
        block = w_ref[:, b * DH : (b + 1) * DH].astype(F32) - iterates[b].astype(F32).T
        w2_ref[:, b * DH : (b + 1) * DH] = block.astype(BF16)
    nw_ref[...] = w2_ref[pl.ds(pl.multiple_of(index_ref[0] * 64, 64), 64), :]
    chunk = 8
    rows = chunk * 64
    for c in range(32 // chunk):
        queries = q_ref[c * chunk : (c + 1) * chunk].reshape(rows, DH)
        gate = mm_nt(queries, w2_ref[:, 0:DH])
        up = mm_nt(queries, w2_ref[:, DH : 2 * DH])
        hidden = (gate * sigmoid(gate) * up).astype(BF16)
        applied = rms_norm(mm(hidden, w2_ref[:, 2 * DH : 3 * DH]))
        ref, at = (first_ref, c * rows) if c < 2 else (second_ref, (c - 2) * rows)
        out_ref[c * chunk : (c + 1) * chunk] = (ref[at : at + rows, :] + applied).astype(BF16).reshape(chunk, 64, DH)


def update_and_apply(index, pieces, weights, query_rows, first, second):
    vmem = pl.BlockSpec(memory_space=pltpu.VMEM)
    return pl.pallas_call(
        update_kernel,
        in_specs=[pl.BlockSpec(memory_space=pltpu.SMEM)] + [vmem] * 8,
        out_specs=[vmem, vmem],
        out_shape=[jax.ShapeDtypeStruct((32, 64, DH), BF16), jax.ShapeDtypeStruct((64, 3 * DH), BF16)],
        scratch_shapes=[pltpu.VMEM((3 * DH, FH), BF16), pltpu.VMEM((FH, 3 * DH), BF16)],
        compiler_params=pltpu.CompilerParams(vmem_limit_bytes=40 * 2**20),
        cost_estimate=pl.CostEstimate(flops=2**33, bytes_accessed=8 * 2**20, transcendentals=2**20),
        name="update",
    )(index, *pieces, weights, query_rows, first, second)


def by_head(states):
    return states.reshape(64, 32, DH).transpose(1, 0, 2)


def exchange(pieces):
    return lax.all_to_all(pieces, "head", split_axis=0, concat_axis=0, tiled=True)


def around(value, axis, steps):
    count = lax.axis_size(axis)
    return lax.ppermute(value, axis, [(k, (k + steps) % count) for k in range(count)])


def per_device(query_states, key_states, value_states, token_rates, fast_weights):
    kv = exchange(jnp.concatenate([by_head(key_states), by_head(value_states)], axis=1))
    query_states, kv = lax.optimization_barrier((query_states, kv))
    query_rows = exchange(by_head(query_states))
    tok_count = lax.axis_size(TOK)
    halo = lax.ppermute(kv[16:32], TOK, [(k, k + 1) for k in range(tok_count - 1)])
    index = jnp.stack([lax.axis_index(TOK), lax.axis_index("tok_1")]).astype(jnp.int32)
    weights = fast_weights[0]
    own, *sends = gradient_pieces(index, kv, weights, token_rates.reshape(16, 128))
    summed = own
    for d in range(1, RING):
        summed = summed + around(sends[d - 1], "tok_1", d).astype(F32)
    summed = summed.astype(BF16)
    other = around(summed, "tok_0", 1)
    summed = (summed.astype(F32) + other.astype(F32)).astype(BF16)
    pieces = [summed] + [around(summed, "tok_1", d) for d in range(1, RING)]
    second = attention(index, query_rows, 1, kv, 0, kv, 1, False)
    first = attention(index, query_rows, 0, halo, 0, kv, 0, True)
    combined, owned = update_and_apply(index, pieces, weights, query_rows, first, second)
    combined = exchange(combined).transpose(1, 0, 2).reshape(64, 32 * DH)
    return (combined, owned[None])


def solution(mesh):
    finer = Mesh(mesh.devices.reshape(2, RING, mesh.shape["head"]), ("tok_0", "tok_1", "head"))
    return jax.shard_map(
        per_device,
        mesh=finer,
        in_specs=(
            P(TOK_HEAD, None),
            P(TOK_HEAD, None),
            P(TOK_HEAD, None),
            P("head", TOK),
            P("head", None, None),
        ),
        out_specs=(P(TOK_HEAD, None), P("head", TOK, None)),
        check_vma=False,
    )
```

time: 283 us -> 199 us (0.70)
  waiting for transfers between devices: 134 us -> 28.2 us
  blocking collectives: 19.2 us -> 120 us
  matrix products: 38.2 us -> 0 us
  Pallas kernels: 0 us -> 19.2 us
  local copies, waits for them, and re-layouts: 23.3 us -> 5.04 us
  between operations: 14.4 us -> 0.76 us
  starting transfers between devices: 37.5 us -> 25.4 us
  other arithmetic: 12.3 us -> 0.44 us
  loops' own time: 2.85 us -> 0 us
    all_to_all x0 -> x2, blocking collectives: none -> 120 us  [exchange(): lax.all_to_all(pieces, 'head', split_axis=0, concat_axis=0, tiled=True)]
    all_to_all x4 -> x1, waiting for transfers between devices: 84 us -> 0.01 us  [exchange(): lax.all_to_all(pieces, 'head', split_axis=0, concat_axis=0, tiled=True)]
    reduce_scatter x2 -> x0, waiting for transfers between devices: 49.5 us -> none  [own_block(): pieces = lax.psum_scatter(pieces, axes[k], scatter_dimension=0, tiled=True)]
    dot_general x26 -> x0, matrix products: 38.2 us -> none  [the longest x4 10.1 us: attend(): jnp.dot(query_rows, key_rows.T, preferred_element_type=jnp.float32)]
    ppermute x2 -> x8, waiting for transfers between devices: 0.13 us -> 28.2 us  [the longest x7 28.2 us: around(): lax.ppermute(value, axis, [(k, (k + steps) % count) for k in range(count)])]
    all_to_all x4 -> x1, starting transfers between devices: 29.6 us -> 4.04 us  [exchange(): lax.all_to_all(pieces, 'head', split_axis=0, concat_axis=0, tiled=True)]
    pallas_call x0 -> x4, Pallas kernels: none -> 19.2 us  [the longest x1 6.75 us: update_and_apply(): pl.pallas_call(update_kernel, in_specs=[pl.BlockSpec(memory_space=pltpu.S...]
    all_gather x2 -> x0, blocking collectives: 19.2 us -> none  [all_blocks(): pieces = lax.all_gather(pieces, axes[k], axis=0, tiled=True)]
  transfers between devices with their start and end apart: 8 -> 9, of which waited for: 6 -> 5; matrix products, arithmetic and copies ran while one was open for 13% -> 1% of each run, Pallas kernels for 0% -> 6%
where the time goes in v1:
time: 199 us
  blocking collectives  120 us (60%)
  waiting for transfers between devices  28.2 us (14%)
  starting transfers between devices  25.4 us (13%)
  Pallas kernels  19.2 us (10%)
  local copies, waits for them, and re-layouts  5.04 us (3%)
    all_to_all x2, blocking collectives, exchange(): lax.all_to_all(pieces, 'head', split_axis=0, concat_axis=0, tiled=True)  120 us
    ppermute x7, waiting for transfers between devices, around(): lax.ppermute(value, axis, [(k, (k + steps) % count) for k in range(count)])  28.2 us
    ppermute x7, starting transfers between devices, around(): lax.ppermute(value, axis, [(k, (k + steps) % count) for k in range(count)])  17.3 us
    pallas_call x1, Pallas kernels, update_and_apply(): pl.pallas_call(update_kernel, in_specs=[pl.BlockSpec(memory_space=pltpu.S...  6.75 us
    pallas_call x2, Pallas kernels, attention(): pl.pallas_call(functools.partial(attention_kernel, check=check), grid=(1,...  6.69 us
    pallas_call x1, Pallas kernels, gradient_pieces(): pl.pallas_call(gradient_kernel, in_specs=[pl.BlockSpec(memory_space=pltpu...  5.75 us
    ppermute x1, starting transfers between devices, per_device(): lax.ppermute(kv[16:32], TOK, [(k, k + 1) for k in range(tok_count - 1)])  4.1 us
    all_to_all x1, starting transfers between devices, exchange(): lax.all_to_all(pieces, 'head', split_axis=0, concat_axis=0, tiled=True)  4.04 us
  transfers between devices with their start and end apart: 9, of which 5 were waited for; matrix products, arithmetic and copies ran while one was open for 1% of the time, Pallas kernels for 6%

profile of v1, /device:TPU:1, one launch (start us, length us, event | category | flops | bytes accessed | tf_op | source)
XLA Modules:
  0.0 198.9 jit_solution(4802806205522362753)
XLA Ops:
  0.6 1.8 bitcast_bitcast_fusion.1
  2.4 0.2 pad_maximum_fusion
  2.7 0.0 copy-start.3
  2.7 60.4 %all_to_all.15.kv_ref.own_ref.prev_ref = bf16[32,128,256]{2,1,0:T(8,128)(2,1)S(1)} all-to-all(bf16[32,128,256]{2,1,0:T(8,128)(2,1)S(1)} %pad_maximum_fusion), channel_id=1, replica_groups=mesh['tok_0'=2,'tok_1'=4,'head'=32] {'head'}, dimensions={0} | all-to-all | bytes 4194304 | tf_op jit(solution)/shard_map/all_to_all | solution.py:201
  63.1 0.0 copy-done.3
  63.1 1.1 copy.18
  64.2 0.0 copy-start.2
  64.2 4.0 %all-to-all-start.1 = ((bf16[32,64,256]{2,1,0:T(8,128)(2,1)}), bf16[32,64,256]{2,1,0:T(8,128)(2,1)S(1)}, u32[]{:S(2)}, u32[]{:S(2)}) async-start(bf16[32,64,256]{2,1,0:T(8,128)(2,1)} %bitcast.28), calls=%async_computation.1 | async-start | bytes 2097152 | tf_op jit(solution)/shard_map/all_to_all | solution.py:201
  68.3 0.0 copy-start
  68.3 0.1 pad_add_fusion.index_ref
  68.3 1.1 slice.3
  69.4 4.1 %collective-permute-start.7 = (bf16[16,128,256]{2,1,0:T(8,128)(2,1)}, bf16[16,128,256]{2,1,0:T(8,128)(2,1)}, u32[]{:S(2)}, u32[]{:S(2)}) collective-permute-start(bf16[16,128,256]{2,1,0:T(8,128)(2,1)} %slice.3), channel_id=1, source_target_pairs={{0,32},{32,64},{64,96},{96,128},{128,160},{160,192},{192,224},{1,3... | collective-permute-start | bytes 3145736 | tf_op jit(solution)/shard_map/ppermute | solution.py:214
  73.5 0.0 copy-done.2
  73.5 0.0 copy-done
  73.5 5.7 %gradient.1 = (f32[192,512]{1,0:T(8,128)S(1)}, bf16[192,512]{1,0:T(8,128)(2,1)S(1)}, bf16[192,512]{1,0:T(8,128)(2,1)S(1)}, bf16[192,512]{1,0:T(8,128)(2,1)S(1)}) custom-call(s32[2]{0:T(128)S(1)} %pad_add_fusion.index_ref, bf16[32,128,256]{2,1,0:T(8,128)(2,1)S(1)} %all_to_all.15.kv_ref.own_ref.prev_ref, bf16[512,768]{1,0:T(8,128)(2,1)S(1)} %bitcast.25, ...), custom_call_target="tpu_custom_call" | custom-call | flops 3221225472 | bytes 4194304 | tf_op jit(solution)/shard_map/gradient/pallas_call | solution.py:89
  79.3 4.5 %collective-permute-start.2 = (bf16[192,512]{1,0:T(8,128)(2,1)S(1)}, bf16[192,512]{1,0:T(8,128)(2,1)S(1)}, u32[]{:S(2)}, u32[]{:S(2)}) collective-permute-start(bf16[192,512]{1,0:T(8,128)(2,1)S(1)} %get-tuple-element.14), channel_id=1, source_target_pairs={{0,96},{32,0},{64,32},{96,64},{1,97},{33,1},{65,33},{97,65},{2,98}... | collective-permute-start | bytes 589832 | tf_op jit(solution)/shard_map/ppermute | solution.py:206
  83.8 0.0 collective-permute-start.1
  83.8 0.7 collective-permute-start
  84.5 7.6 %collective-permute-done.2 = bf16[192,512]{1,0:T(8,128)(2,1)S(1)} collective-permute-done((bf16[192,512]{1,0:T(8,128)(2,1)S(1)}, bf16[192,512]{1,0:T(8,128)(2,1)S(1)}, u32[]{:S(2)}, u32[]{:S(2)}) %collective-permute-start.2) | collective-permute-done | bytes 196640 | tf_op jit(solution)/shard_map/ppermute | solution.py:206
  92.0 10.4 %collective-permute-done.1 = bf16[192,512]{1,0:T(8,128)(2,1)S(1)} collective-permute-done((bf16[192,512]{1,0:T(8,128)(2,1)S(1)}, bf16[192,512]{1,0:T(8,128)(2,1)S(1)}, u32[]{:S(2)}, u32[]{:S(2)}) %collective-permute-start.1) | collective-permute-done | bytes 196640 | tf_op jit(solution)/shard_map/ppermute | solution.py:206
  102.4 1.1 collective-permute-done
  103.5 0.1 add_convert_fusion.1
  103.6 8.7 %collective-permute-start.3 = (bf16[192,512]{1,0:T(8,128)(2,1)S(1)}, bf16[192,512]{1,0:T(8,128)(2,1)S(1)}, u32[]{:S(2)}, u32[]{:S(2)}) collective-permute-start(bf16[192,512]{1,0:T(8,128)(2,1)S(1)} %add_convert_fusion.1), channel_id=1, source_target_pairs={{0,128},{128,0},{1,129},{129,1},{2,130},{130,2},{3,131},{131,3},{4... | collective-permute-start | bytes 589832 | tf_op jit(solution)/shard_map/ppermute | solution.py:206
  112.2 8.8 %collective-permute-done.3 = bf16[192,512]{1,0:T(8,128)(2,1)S(1)} collective-permute-done((bf16[192,512]{1,0:T(8,128)(2,1)S(1)}, bf16[192,512]{1,0:T(8,128)(2,1)S(1)}, u32[]{:S(2)}, u32[]{:S(2)}) %collective-permute-start.3) | collective-permute-done | bytes 196640 | tf_op jit(solution)/shard_map/ppermute | solution.py:206
  121.1 0.1 add_convert_fusion.p0_ref
  121.1 0.1 collective-permute-start.4
  121.2 3.3 %collective-permute-start.5 = (bf16[192,512]{1,0:T(8,128)(2,1)S(1)}, bf16[192,512]{1,0:T(8,128)(2,1)}, u32[]{:S(2)}, u32[]{:S(2)}) collective-permute-start(bf16[192,512]{1,0:T(8,128)(2,1)S(1)} %add_convert_fusion.p0_ref), channel_id=1, source_target_pairs={{0,64},{32,96},{64,0},{96,32},{1,65},{33,97},{65,1},{97,33},{2,66}... | collective-permute-start | bytes 589832 | tf_op jit(solution)/shard_map/ppermute | solution.py:206
  124.6 0.0 collective-permute-start.6
  124.6 0.0 all-to-all-done.1.q_ref
  124.6 3.0 %attention.3.second_ref = f32[1024,256]{1,0:T(8,128)S(1)} custom-call(s32[2]{0:T(128)S(1)} %pad_add_fusion.index_ref, bf16[32,64,256]{2,1,0:T(8,128)(2,1)S(1)} %all-to-all-done.1.q_ref, bf16[32,128,256]{2,1,0:T(8,128)(2,1)S(1)} %all_to_all.15.kv_ref.own_ref.prev_ref, bf16[32,128,256]{2,1,0:T(8,128)(2,1)S(1)} %all_to_all.15.kv_ref.own_ref.prev_ref), custom_call_target="tpu_custom_call" | custom-call | flops 1342177280 | bytes 4194304 | tf_op jit(solution)/shard_map/attention/pallas_call | solution.py:135
  127.5 0.0 copy-start.1
  127.5 0.0 collective-permute-done.7.prev_ref
  127.5 3.7 %attention.2.first_ref = f32[1024,256]{1,0:T(8,128)S(1)} custom-call(s32[2]{0:T(128)S(1)} %pad_add_fusion.index_ref, bf16[32,64,256]{2,1,0:T(8,128)(2,1)S(1)} %all-to-all-done.1.q_ref, bf16[16,128,256]{2,1,0:T(8,128)(2,1)} %collective-permute-done.7.prev_ref, bf16[32,128,256]{2,1,0:T(8,128)(2,1)S(1)} %all_to_all.15.kv_ref.own_ref.prev_ref), custom_call_target="tpu_custom_call" | custom-call | flops 1342177280 | bytes 4194304 | tf_op jit(solution)/shard_map/attention/pallas_call | solution.py:135
  131.3 0.0 collective-permute-done.4.p1_ref
  131.3 0.0 collective-permute-done.5.p2_ref
  131.3 0.4 collective-permute-done.6.p3_ref
  131.7 0.0 copy-done.1
  131.7 6.7 %update.1 = (bf16[32,64,256]{2,1,0:T(8,128)(2,1)S(1)}, bf16[64,768]{1,0:T(8,128)(2,1)}) custom-call(s32[2]{0:T(128)S(1)} %pad_add_fusion.index_ref, bf16[192,512]{1,0:T(8,128)(2,1)S(1)} %add_convert_fusion.p0_ref, bf16[192,512]{1,0:T(8,128)(2,1)S(1)} %collective-permute-done.4.p1_ref, bf16[192,512]{1,0:T(8,128)(2,1)} %collective-permute-done.5.p2_ref, ...), custom_call_target="tpu_custom_call" | custom-call | flops 8589934592 | bytes 8388608 | tf_op jit(solution)/shard_map/update/pallas_call | solution.py:184
  138.5 59.4 %all_to_all.16 = bf16[32,64,256]{2,1,0:T(8,128)(2,1)S(1)} all-to-all(bf16[32,64,256]{2,1,0:T(8,128)(2,1)S(1)} %get-tuple-element.16), channel_id=1, replica_groups=mesh['tok_0'=2,'tok_1'=4,'head'=32] {'head'}, dimensions={0} | all-to-all | bytes 2097152 | tf_op jit(solution)/shard_map/all_to_all | solution.py:201
  197.8 1.0 copy.14
Async XLA Ops:
  2.7 60.4 %copy-start.3 = (bf16[64,8192]{1,0:T(8,128)(2,1)S(1)}, bf16[64,8192]{1,0:T(8,128)(2,1)}, u32[]{:S(2)}) copy-start(bf16[64,8192]{1,0:T(8,128)(2,1)} %param.5) | copy-start | bytes 3145732
  64.2 9.3 %copy-start.2 = (f32[1,2048]{1,0:T(1,128)S(1)}, f32[1,2048]{1,0:T(1,128)}, u32[]{:S(2)}) copy-start(f32[1,2048]{1,0:T(1,128)} %param.8) | copy-start | bytes 24580
  64.2 60.3 %all-to-all-start.1 = ((bf16[32,64,256]{2,1,0:T(8,128)(2,1)}), bf16[32,64,256]{2,1,0:T(8,128)(2,1)S(1)}, u32[]{:S(2)}, u32[]{:S(2)}) async-start(bf16[32,64,256]{2,1,0:T(8,128)(2,1)} %bitcast.28), calls=%async_computation.1 | async-start | bytes 2097152 | tf_op jit(solution)/shard_map/all_to_all | solution.py:201
  68.3 5.3 %copy-start = (bf16[1,512,768]{2,1,0:T(8,128)(2,1)S(1)}, bf16[1,512,768]{2,1,0:T(8,128)(2,1)}, u32[]{:S(2)}) copy-start(bf16[1,512,768]{2,1,0:T(8,128)(2,1)} %param.9) | copy-start | bytes 2359300
  69.4 58.1 %collective-permute-start.7 = (bf16[16,128,256]{2,1,0:T(8,128)(2,1)}, bf16[16,128,256]{2,1,0:T(8,128)(2,1)}, u32[]{:S(2)}, u32[]{:S(2)}) collective-permute-start(bf16[16,128,256]{2,1,0:T(8,128)(2,1)} %slice.3), channel_id=1, source_target_pairs={{0,32},{32,64},{64,96},{96,128},{128,160},{160,192},{192,224},{1,3... | collective-permute-start | bytes 3145736 | tf_op jit(solution)/shard_map/ppermute | solution.py:214
  79.3 12.7 %collective-permute-start.2 = (bf16[192,512]{1,0:T(8,128)(2,1)S(1)}, bf16[192,512]{1,0:T(8,128)(2,1)S(1)}, u32[]{:S(2)}, u32[]{:S(2)}) collective-permute-start(bf16[192,512]{1,0:T(8,128)(2,1)S(1)} %get-tuple-element.14), channel_id=1, source_target_pairs={{0,96},{32,0},{64,32},{96,64},{1,97},{33,1},{65,33},{97,65},{2,98}... | collective-permute-start | bytes 589832 | tf_op jit(solution)/shard_map/ppermute | solution.py:206
  83.8 18.6 %collective-permute-start.1 = (bf16[192,512]{1,0:T(8,128)(2,1)S(1)}, bf16[192,512]{1,0:T(8,128)(2,1)S(1)}, u32[]{:S(2)}, u32[]{:S(2)}) collective-permute-start(bf16[192,512]{1,0:T(8,128)(2,1)S(1)} %get-tuple-element.13), channel_id=1, source_target_pairs={{0,64},{32,96},{64,0},{96,32},{1,65},{33,97},{65,1},{97,33},{2,66}... | collective-permute-start | bytes 589832 | tf_op jit(solution)/shard_map/ppermute | solution.py:206
  83.8 19.7 %collective-permute-start = (bf16[192,512]{1,0:T(8,128)(2,1)S(1)}, bf16[192,512]{1,0:T(8,128)(2,1)S(1)}, u32[]{:S(2)}, u32[]{:S(2)}) collective-permute-start(bf16[192,512]{1,0:T(8,128)(2,1)S(1)} %get-tuple-element.12), channel_id=1, source_target_pairs={{0,32},{32,64},{64,96},{96,0},{1,33},{33,65},{65,97},{97,1},{2,34}... | collective-permute-start | bytes 589832 | tf_op jit(solution)/shard_map/ppermute | solution.py:206
  103.6 17.5 %collective-permute-start.3 = (bf16[192,512]{1,0:T(8,128)(2,1)S(1)}, bf16[192,512]{1,0:T(8,128)(2,1)S(1)}, u32[]{:S(2)}, u32[]{:S(2)}) collective-permute-start(bf16[192,512]{1,0:T(8,128)(2,1)S(1)} %add_convert_fusion.1), channel_id=1, source_target_pairs={{0,128},{128,0},{1,129},{129,1},{2,130},{130,2},{3,131},{131,3},{4... | collective-permute-start | bytes 589832 | tf_op jit(solution)/shard_map/ppermute | solution.py:206
  121.1 10.1 %collective-permute-start.4 = (bf16[192,512]{1,0:T(8,128)(2,1)S(1)}, bf16[192,512]{1,0:T(8,128)(2,1)S(1)}, u32[]{:S(2)}, u32[]{:S(2)}) collective-permute-start(bf16[192,512]{1,0:T(8,128)(2,1)S(1)} %add_convert_fusion.p0_ref), channel_id=1, source_target_pairs={{0,32},{32,64},{64,96},{96,0},{1,33},{33,65},{65,97},{97,1},{2,34}... | collective-permute-start | bytes 589832 | tf_op jit(solution)/shard_map/ppermute | solution.py:206
  121.2 10.1 %collective-permute-start.5 = (bf16[192,512]{1,0:T(8,128)(2,1)S(1)}, bf16[192,512]{1,0:T(8,128)(2,1)}, u32[]{:S(2)}, u32[]{:S(2)}) collective-permute-start(bf16[192,512]{1,0:T(8,128)(2,1)S(1)} %add_convert_fusion.p0_ref), channel_id=1, source_target_pairs={{0,64},{32,96},{64,0},{96,32},{1,65},{33,97},{65,1},{97,33},{2,66}... | collective-permute-start | bytes 589832 | tf_op jit(solution)/shard_map/ppermute | solution.py:206
  124.6 7.1 %collective-permute-start.6 = (bf16[192,512]{1,0:T(8,128)(2,1)S(1)}, bf16[192,512]{1,0:T(8,128)(2,1)}, u32[]{:S(2)}, u32[]{:S(2)}) collective-permute-start(bf16[192,512]{1,0:T(8,128)(2,1)S(1)} %add_convert_fusion.p0_ref), channel_id=1, source_target_pairs={{0,96},{32,0},{64,32},{96,64},{1,97},{33,1},{65,33},{97,65},{2,98}... | collective-permute-start | bytes 589832 | tf_op jit(solution)/shard_map/ppermute | solution.py:206
  127.5 4.2 %copy-start.1 = (bf16[1,512,768]{2,1,0:T(8,128)(2,1)S(1)}, bf16[1,512,768]{2,1,0:T(8,128)(2,1)}, u32[]{:S(2)}) copy-start(bf16[1,512,768]{2,1,0:T(8,128)(2,1)} %param.9) | copy-start | bytes 2359300
